TPU v7x, 256 devices: a whole 4x4x8 slice. The times are simulated.
256 devices in a mesh: orb: 16 (over y, x_lo, core), walk: 16 (over z, x_hi).
Axes of the slice: x: 4 (x_hi: 2, x_lo: 2; x = x_hi * 2 + x_lo), y: 4, z: 8, core: 2. Of those that a mesh axis runs over, the one named last changes fastest.
Arguments:
- chol: bfloat16 [64, 2048, 2048], P(None, 'orb', 'walk'), may hold values from -6 to 6
- orbitals: bfloat16 [2048, 1024], replicated, may hold values from -0.125 to 0.125
- greens: bfloat16 [16, 1024, 2048], P('walk'), may hold values from -0.00390625 to 0.00390625
- shift: float32 [64], P('orb'), may hold values from -6 to 6
Outputs:
- force_bias: float32 [16, 64], P('walk', 'orb')
- rotated: bfloat16 [64, 1024, 2048], P('orb', None, 'walk')
All inputs are finite; a program needn't handle non-finite values.
Results may differ from a plain program's by a relative error of at most 0.007.
Values may be sent and summed in bfloat16 or wider, within the bound.
A program may use at most 64 MiB of HBM per device.

v0:
```python
import jax
import jax.numpy as jnp
from jax import lax
from jax.sharding import Mesh
from jax.sharding import PartitionSpec as P

WALK = ("walk_0", "walk_1")


def split_up(array, dim, length):
    dims = array.shape
    tiles = array.reshape(*dims[:dim], length, dims[dim] // length, *dims[dim + 1 :])
    return jnp.moveaxis(tiles, dim, 0)


def sent_and_summed(array, axis, dim):
    tiles = split_up(array, dim, lax.axis_size(axis))
    arrived = lax.all_to_all(tiles, axis, split_axis=0, concat_axis=0, tiled=True)
    return arrived.sum(axis=0)


def summed_rows(array, axes, dim):
    if not axes:
        return array
    nearer = lax.psum_scatter(array, axes[0], scatter_dimension=dim, tiled=True)
    return summed_rows(nearer, axes[1:], dim)


def local(chol, orbitals, greens, shift):
    regrouped = lax.all_to_all(chol, "orb", split_axis=0, concat_axis=1, tiled=True)
    rotation = jnp.einsum("pi,gpq->giq", orbitals, regrouped, preferred_element_type=jnp.float32)
    rotated = rotation.astype(jnp.bfloat16)
    row_count = chol.shape[1]
    row_start = lax.axis_index("orb") * row_count
    orbital_rows = lax.dynamic_slice_in_dim(orbitals, row_start, row_count, 0)
    products = jnp.einsum("pi,wiq->wpq", orbital_rows, greens, preferred_element_type=jnp.float32)
    arrived = lax.all_to_all(
        products.astype(jnp.bfloat16), WALK, split_axis=2, concat_axis=0, tiled=True
    ).astype(products.dtype)
    terms = jnp.einsum(
        "wpq,gpq->wg", arrived, chol.astype(jnp.float32), precision=lax.Precision.HIGHEST
    )
    by_vector = sent_and_summed(terms, "orb", 1)
    totals = summed_rows(by_vector, WALK, 0)
    return (totals - shift[None, :], rotated)


def solution(mesh):
    split = Mesh(mesh.devices.reshape(mesh.shape["orb"], 8, 2), ("orb", "walk_0", "walk_1"))
    placed = (P(None, "orb", WALK), P(), P(WALK, None, None), P("orb"))
    return jax.shard_map(
        local,
        mesh=split,
        in_specs=placed,
        out_specs=(P(WALK, "orb"), P("orb", None, WALK)),
        check_vma=False,
    )
```

profile of v0, /device:TPU:1, one launch (start us, length us, event | category | flops | bytes accessed | tf_op | source)
XLA Modules:
  0.0 105.8 jit_solution(9569453048938071418)
XLA Ops:
  0.6 3.0 %fusion.7 = bf16[1,128,2048]{2,1,0:T(8,128)(2,1)S(1)} fusion(bf16[1,1024,2048]{2,1,0:T(8,128)(2,1)} %param.6, bf16[2048,1024]{1,0:T(8,128)(2,1)} %param.5, s32[]{:T(128)S(6)} %select_n.3), kind=kOutput, calls=%fused_computation.5 | convolution fusion | flops 537133056 | bytes 4980740 | tf_op jit(solution)/shard_map/pi,wiq->wpq/dot_general | solution.py:36
  3.6 0.8 copy.9
  4.4 0.5 broadcast
  4.9 11.5 %reduce = bf16[2048,128]{1,0:T(8,128)(2,1)S(1)} reduce(bf16[2048,1,128]{2,1,0:T(2,128)(2,1)S(1)} %bitcast.52, bf16[]{:T(256)} %broadcast), dimensions={1}, to_apply=%bitcast.46.reduce_sub_computation | reduce | bytes 1048578
  16.5 0.1 reshape.18
  16.6 28.6 %all_to_all.41 = bf16[16,2,8192]{2,1,0:T(2,128)(2,1)S(1)} all-to-all(bf16[16,2,8192]{2,1,0:T(2,128)(2,1)S(1)} %reshape.18), channel_id=1, replica_groups=mesh['orb'=16,'walk_0'=8,'walk_1'=2] {'walk_0','walk_1'}, dimensions={0} | all-to-all | bytes 1048576 | tf_op jit(solution)/shard_map/all_to_all | solution.py:37
  45.2 0.5 reshape.19
  45.7 0.1 copy.19
  45.8 0.4 copy.18
  46.2 4.1 %fusion.18 = f32[16,16,4]{0,1,2:T(8,128)S(1)} fusion(bf16[16,4,128,128]{3,2,1,0:T(8,128)(2,1)} %bitcast.54, bf16[1,128,16,128]{3,2,1,0:T(8,128)(2,1)S(1)} %copy.18), kind=kOutput, calls=%fused_computation.10 | convolution fusion | flops 33554432 | bytes 2625536 | tf_op jit(solution)/shard_map/wpq,gpq->wg/dot_general | solution.py:40
  50.3 0.1 copy.12
  50.4 12.7 %all_to_all.42 = f32[16,16,4]{1,2,0:T(4,128)S(1)} all-to-all(f32[16,16,4]{1,2,0:T(4,128)S(1)} %copy.12), channel_id=1, replica_groups=mesh['orb'=16,'walk_0'=8,'walk_1'=2] {'orb'}, dimensions={0} | all-to-all | bytes 8192 | tf_op jit(solution)/shard_map/all_to_all | solution.py:18
  63.1 4.0 %all-to-all-start.2 = ((bf16[64,128,128]{2,1,0:T(8,128)(2,1)}), bf16[64,128,128]{2,1,0:T(8,128)(2,1)S(1)}, u32[]{:S(2)}, u32[]{:S(2)}) async-start(bf16[64,128,128]{2,1,0:T(8,128)(2,1)} %param.4), calls=%async_computation.2 | async-start | bytes 4194304 | tf_op jit(solution)/shard_map/all_to_all | solution.py:30
  67.1 0.6 dynamic-slice
  68.4 0.1 copy.14
  68.5 12.1 %all-reduce = f32[16,4]{1,0:T(8,128)S(1)} all-reduce(f32[16,4]{1,0:T(8,128)S(1)} %copy.14), channel_id=2, replica_groups=mesh['orb'=16,'walk_0'=8,'walk_1'=2] {'walk_0'}, use_global_device_ids=true, to_apply=%region_1.0.clone | all-reduce | flops 64 | bytes 512
  80.6 0.6 dynamic-slice.2
  81.2 10.9 %all-reduce.1 = f32[2,4]{1,0:T(2,128)S(1)} all-reduce(f32[2,4]{1,0:T(2,128)S(1)} %constant_dynamic-slice_fusion.1), channel_id=3, replica_groups=mesh['orb'=16,'walk_0'=8,'walk_1'=2] {'walk_1'}, use_global_device_ids=true, to_apply=%region_2.0.clone | all-reduce | flops 8 | bytes 64
  92.1 1.2 %fusion.23 = f32[1,4]{1,0:T(1,128)} fusion(f32[2,4]{1,0:T(2,128)S(1)} %all-reduce.1, u32[]{:T(128)} %bitcast.22, f32[4]{0:T(128)S(1)} %copy-done), kind=kLoop, calls=%fused_computation.15 | loop fusion | flops 4 | bytes 52 | tf_op jit(solution)/shard_map/sub | solution.py:45
  93.2 0.9 all-to-all-done.2
  94.2 2.9 %copy.15 = bf16[16,4,128,128]{2,0,3,1:T(8,128)(2,1)} copy(bf16[16,4,128,128]{3,2,1,0:T(8,128)(2,1)S(1)} %bitcast.49) | data formatting | bytes 4194304 | tf_op jit(solution)/shard_map/all_to_all | solution.py:30
  97.1 2.8 %all_to_all.37 = bf16[4,2048,128]{1,2,0:T(8,128)(2,1)S(1)} reshape(bf16[4,16,128,128]{2,1,3,0:T(8,128)(2,1)} %bitcast.50) | data formatting | bytes 4194304 | tf_op jit(solution)/shard_map/all_to_all | solution.py:30
  99.9 4.5 %fusion.15 = bf16[4,1024,128]{1,2,0:T(8,128)(2,1)S(1)} fusion(bf16[4,2048,128]{1,2,0:T(8,128)(2,1)S(1)} %all_to_all.37, bf16[2048,1024]{1,0:T(8,128)(2,1)} %param.5), kind=kOutput, calls=%fused_computation.9 | convolution fusion | flops 2148007936 | bytes 7340032 | tf_op jit(solution)/shard_map/pi,gpq->giq/dot_general | solution.py:31
  104.4 1.3 %copy.16 = bf16[4,1024,128]{2,1,0:T(8,128)(2,1)} copy(bf16[4,1024,128]{1,2,0:T(8,128)(2,1)S(1)} %fusion.15) | data formatting | bytes 2097152
  (8 shorter events, 0.1 us)
Async XLA Ops:
  63.1 4.0 %copy-start.2 = (u32[256]{0:T(256)S(1)}, u32[256]{0:T(256)}, u32[]{:S(2)}) copy-start(u32[256]{0:T(256)} %constant.17) | copy-start | bytes 3076
  63.1 17.5 %copy-start.1 = (u32[256]{0:T(256)S(1)}, u32[256]{0:T(256)}, u32[]{:S(2)}) copy-start(u32[256]{0:T(256)} %constant.21) | copy-start | bytes 3076
  63.1 29.0 %copy-start = (f32[4]{0:T(128)S(1)}, f32[4]{0:T(128)}, u32[]{:S(2)}) copy-start(f32[4]{0:T(128)} %param.7) | copy-start | bytes 52
  63.1 31.1 %all-to-all-start.2 = ((bf16[64,128,128]{2,1,0:T(8,128)(2,1)}), bf16[64,128,128]{2,1,0:T(8,128)(2,1)S(1)}, u32[]{:S(2)}, u32[]{:S(2)}) async-start(bf16[64,128,128]{2,1,0:T(8,128)(2,1)} %param.4), calls=%async_computation.2 | async-start | bytes 4194304 | tf_op jit(solution)/shard_map/all_to_all | solution.py:30
where the time goes:
time: 106 us
  blocking collectives  64.2 us (61%)
  other arithmetic  12.7 us (12%)
  matrix products  11.7 us (11%)
  local copies, waits for them, and re-layouts  10.8 us (10%)
  starting transfers between devices  4.04 us (4%)
  between operations  1.39 us (1%)
    all_to_all x1, blocking collectives, local(): lax.all_to_all(products.astype(jnp.bfloat16), WALK, split_axis=2, concat_...  28.6 us
    unnamed x2, blocking collectives  23 us
    all_to_all x1, blocking collectives, sent_and_summed(): lax.all_to_all(tiles, axis, split_axis=0, concat_axis=0, tiled=True)  12.7 us
    unnamed x1, other arithmetic  11.5 us
    all_to_all x2, local copies, waits for them, and re-layouts, local(): lax.all_to_all(chol, 'orb', split_axis=0, concat_axis=1, tiled=True)  5.74 us
    dot_general x1, matrix products, local(): jnp.einsum('pi,gpq->giq', orbitals, regrouped, preferred_element_type=jnp...  4.52 us
    dot_general x1, matrix products, local(): jnp.einsum('wpq,gpq->wg', arrived, chol.astype(jnp.float32), precision=la...  4.14 us
    all_to_all x1, starting transfers between devices, local(): lax.all_to_all(chol, 'orb', split_axis=0, concat_axis=1, tiled=True)  4.04 us
  transfers between devices with their start and end apart: 1, of which 1 were waited for; matrix products, arithmetic and copies ran while one was open for 2% of the time, Pallas kernels for 0%

commit v1 on v0

v1 whole, which is shorter than its diff:
```python
import jax
import jax.numpy as jnp
from jax import lax
from jax.experimental import pallas as pl
from jax.experimental.pallas import tpu as pltpu
from jax.sharding import PartitionSpec as P

MESH = pl.DeviceIdType.MESH
F32, BF16 = jnp.float32, jnp.bfloat16
FAR_FIRST = (4, 3, 5, 2, 6, 1, 7, 0)
CHIPS = ((0, 0), (1, 0), (3, 0), (2, 0), (2, 1), (1, 1), (3, 1), (0, 1))


def kernel(
    chol, orbitals, greens, shift, fb_out, rot_out,
    rows_v, greens_v, orb_v, orb_t, chol_v, chunks, acc,
    t_out, t_in, diag, part_out, part_in, sum_out, sum_in,
    orb_ready, walk_ready, load_sem, greens_sem,
    chol_send, chol_recv, t_send, t_recv, part_send, part_recv, sum_send, sum_recv,
):
    o, w = lax.axis_index("orb"), lax.axis_index("walk")
    y, a, c = o // 4, (o // 2) % 2, o % 2
    z, h = w // 2, w % 2
    across = y * 4 + (1 - a) * 2 + c
    pair = (o // 2) * 2
    partner = pair + 1 - c

    def place(orb, walk):
        return {"orb": orb, "walk": walk}

    def met(walk):
        return place(jnp.where(walk % 2 == h, o, across), walk)

    def signal(sem, where):
        pl.semaphore_signal(sem, inc=1, device_id=where, device_id_type=MESH)

    def await_some(sem, amount):
        @pl.when(amount > 0)
        def _():
            pl.semaphore_wait(sem, amount)

    def loop(start, stop, body):
        lax.fori_loop(start, stop, lambda i, _: body(i), None)

    barrier = pltpu.get_barrier_semaphore()
    signal(barrier, place(partner, w))
    loop(pair + 2, 16, lambda i: signal(barrier, place(i, w)))
    loop(w + 1, 16, lambda i: signal(barrier, met(i)))

    own_rows = pltpu.make_async_copy(
        orbitals.at[pl.ds(pl.multiple_of(o * 128, 128), 128)], rows_v.at[h], load_sem.at[0]
    )
    far_rows = pltpu.make_async_copy(
        orbitals.at[pl.ds(pl.multiple_of(across * 128, 128), 128)], rows_v.at[1 - h], load_sem.at[1]
    )
    own_rows.start()
    far_rows.start()
    columns = []
    for k, dz in enumerate(FAR_FIRST):
        there = pl.multiple_of(((z + dz) % 8) * 256, 256)
        copy = pltpu.make_async_copy(
            greens.at[0, :, pl.ds(there, 256)], greens_v.at[k], greens_sem.at[k]
        )
        copy.start()
        columns.append(copy)
    all_rows = pltpu.make_async_copy(orbitals, orb_v, load_sem.at[2])
    all_rows.start()
    own_chol = pltpu.make_async_copy(chol, chol_v, load_sem.at[3])
    own_chol.start()
    own_chunk = pltpu.make_async_copy(chol.at[pl.ds(4 * o, 4)], chunks.at[o], load_sem.at[4])
    own_chunk.start()

    pl.semaphore_wait(barrier, pair + 1 + w)
    loop(0, pair, lambda i: signal(orb_ready, place(i, w)))
    loop(0, w, lambda i: signal(walk_ready, met(i)))

    def chunk_copy(to):
        return pltpu.make_async_remote_copy(
            src_ref=chol.at[pl.ds(4 * to, 4)],
            dst_ref=chunks.at[o],
            send_sem=chol_send.at[to],
            recv_sem=chol_recv.at[o],
            device_id=place(to, w),
            device_id_type=MESH,
        )

    def chunk_arrival(source):
        pltpu.make_async_remote_copy(
            src_ref=chol.at[pl.ds(4 * source, 4)],
            dst_ref=chunks.at[source],
            send_sem=chol_send.at[source],
            recv_sem=chol_recv.at[source],
            device_id=place(source, w),
            device_id_type=MESH,
        ).wait_recv()

    def chip(dy, da):
        return ((y + dy) % 4) * 2 + (a + da) % 2

    await_some(orb_ready, 14 - pair)
    for dy, da in ((2, 1), (1, 1), (3, 1), (0, 1), (2, 0), (1, 0), (3, 0)):
        for dc in range(2):
            chunk_copy(chip(dy, da) * 2 + (c + dc) % 2).start()
    chunk_copy(partner).start()

    own_rows.wait()
    far_rows.wait()
    for k, dz in enumerate(FAR_FIRST):
        columns[k].wait()
        there = (z + dz) % 8
        both = jnp.dot(
            rows_v[...].reshape(256, 1024), greens_v[k], preferred_element_type=F32
        ).astype(BF16)
        t_out[2 * there] = both[:128, :128]
        t_out[2 * there + 1] = both[128:, 128:]

    def t_copy(to, source):
        return pltpu.make_async_remote_copy(
            src_ref=t_out.at[to],
            dst_ref=t_in.at[source],
            send_sem=t_send.at[to],
            recv_sem=t_recv.at[source],
            device_id=met(to),
            device_id_type=MESH,
        )

    await_some(walk_ready, 15 - w)
    for dz in FAR_FIRST:
        for dh in (1, 0):
            if dz or dh:
                t_copy(((z + dz) % 8) * 2 + (h + dh) % 2, w).start()
    t_in[w] = t_out[w]

    all_rows.wait()

    def turn(i):
        at = pl.ds(pl.multiple_of(i * 128, 128), 128)
        orb_t[:, at] = orb_v[at, :].T

    loop(0, 16, turn)

    def rotate(which):
        dy, da = CHIPS[which]
        there = chip(dy, da)
        if which == 0:
            own_chunk.wait()
            chunk_arrival(partner)
        else:
            chunk_arrival(2 * there)
            chunk_arrival(2 * there + 1)
        block = jnp.concatenate(
            [
                jnp.concatenate([chunks[2 * there, g], chunks[2 * there + 1, g]], axis=0)
                for g in range(4)
            ],
            axis=1,
        )
        at = pl.ds(pl.multiple_of(there * 256, 256), 256)

        def rows(i):
            here = pl.ds(pl.multiple_of(i * 256, 256), 256)
            term = jnp.dot(orb_t[here, at], block, preferred_element_type=F32)
            if which:
                term = acc[here, :] + term
            if which < 7:
                acc[here, :] = term
            else:
                for g in range(4):
                    rot_out[g, here, :] = term[:, g * 128 : (g + 1) * 128].astype(BF16)

        loop(0, 4, rows)

    lane = lax.broadcasted_iota(jnp.int32, (256, 128), 1)
    row = lax.broadcasted_iota(jnp.int32, (256, 128), 0)
    same_row = (lane % 16) == (row % 16)

    def part_copy(to, source):
        return pltpu.make_async_remote_copy(
            src_ref=part_out.at[to],
            dst_ref=part_in.at[source],
            send_sem=part_send.at[to],
            recv_sem=part_recv.at[source],
            device_id=met(to),
            device_id_type=MESH,
        )

    def terms(first):
        for k in range(first, first + 8):
            @pl.when(w != k)
            def _():
                t_copy(k, k).wait_recv()

        right = jnp.concatenate(
            [t_in[first : first + 8, 16 * b : 16 * b + 16, :].reshape(128, 128) for b in range(8)],
            axis=1,
        )

        def vectors(j):
            at = pl.ds(pl.multiple_of(j * 16, 16), 16)
            left = jnp.concatenate(
                [chol_v[at, 16 * b : 16 * b + 16, :].reshape(256, 128) for b in range(8)],
                axis=1,
            )
            product = lax.dot_general(
                left, right, (((1,), (1,)), ((), ())), preferred_element_type=F32
            )
            kept = jnp.where(same_row, product, 0.0)
            diag[at, :] = kept.reshape(16, 16, 128).sum(axis=1)

        loop(0, 4, vectors)
        picks = jnp.where(
            lax.broadcasted_iota(jnp.int32, (8, 128), 1) // 16
            == lax.broadcasted_iota(jnp.int32, (8, 128), 0),
            1.0, 0.0,
        )
        sums = lax.dot_general(
            picks, diag[...], (((1,), (1,)), ((), ())),
            precision=lax.Precision.HIGHEST, preferred_element_type=F32,
        )
        for k in range(8):
            part_out[first + k] = jnp.broadcast_to(sums[k : k + 1, :], (8, 128))
        for k in range(first, first + 8):
            @pl.when(w != k)
            def _():
                part_copy(k, w).start()

    diag[64:, :] = jnp.zeros((64, 128), F32)
    for which in range(4):
        rotate(which)
    own_chol.wait()
    terms(0)
    rotate(4)
    terms(8)
    rotate(5)
    rotate(6)

    part_in[w] = part_out[w]
    for k in range(16):
        @pl.when(w != k)
        def _():
            part_copy(k, k).wait_recv()

    sum_out[...] = part_in[...].sum(axis=0)

    def sum_copy(to, source):
        return pltpu.make_async_remote_copy(
            src_ref=sum_out,
            dst_ref=sum_in.at[source],
            send_sem=sum_send.at[to],
            recv_sem=sum_recv.at[source],
            device_id=place(to, w),
            device_id_type=MESH,
        )

    for k in range(16):
        @pl.when(o != k)
        def _():
            sum_copy(k, o).start()
    sum_in[o] = sum_out[...]
    rotate(7)
    for k in range(16):
        @pl.when(o != k)
        def _():
            sum_copy(k, k).wait_recv()

    total = pltpu.roll(sum_in[...].sum(axis=0), (128 - 4 * o) % 128, 1)[:1]
    spot = lax.broadcasted_iota(jnp.int32, (1, 128), 1)
    moved = jnp.zeros((1, 128), F32)
    for j in range(4):
        moved = jnp.where(spot == j, shift[j], moved)
    fb_out[...] = (total - moved)[:, :4]

    for k in range(16):
        @pl.when(o != k)
        def _():
            chunk_copy(k).wait_send()
            sum_copy(k, o).wait_send()

        @pl.when(w != k)
        def _():
            t_copy(k, w).wait_send()
            part_copy(k, w).wait_send()


def local(chol, orbitals, greens, shift):
    anywhere = pl.BlockSpec(memory_space=pl.ANY)
    in_vmem = pl.BlockSpec(memory_space=pltpu.VMEM)
    sems = [pltpu.SemaphoreType.DMA((16,))] * 8
    return pl.pallas_call(
        kernel,
        out_shape=(
            jax.ShapeDtypeStruct((1, 4), F32),
            jax.ShapeDtypeStruct((4, 1024, 128), BF16),
        ),
        in_specs=[anywhere, anywhere, anywhere, pl.BlockSpec(memory_space=pltpu.SMEM)],
        out_specs=(in_vmem, in_vmem),
        scratch_shapes=[
            pltpu.VMEM((2, 128, 1024), BF16),
            pltpu.VMEM((8, 1024, 256), BF16),
            pltpu.VMEM((2048, 1024), BF16),
            pltpu.VMEM((1024, 2048), BF16),
            pltpu.VMEM((64, 128, 128), BF16),
            pltpu.VMEM((16, 4, 128, 128), BF16),
            pltpu.VMEM((1024, 512), F32),
            pltpu.VMEM((16, 128, 128), BF16),
            pltpu.VMEM((16, 128, 128), BF16),
            pltpu.VMEM((128, 128), F32),
            pltpu.VMEM((16, 8, 128), F32),
            pltpu.VMEM((16, 8, 128), F32),
            pltpu.VMEM((8, 128), F32),
            pltpu.VMEM((16, 8, 128), F32),
            pltpu.SemaphoreType.REGULAR,
            pltpu.SemaphoreType.REGULAR,
            pltpu.SemaphoreType.DMA((5,)),
            pltpu.SemaphoreType.DMA((8,)),
            *sems,
        ],
        compiler_params=pltpu.CompilerParams(
            collective_id=0, has_side_effects=True, vmem_limit_bytes=62 * 2**20
        ),
        name="half_rotation",
    )(chol, orbitals, greens, shift)


def solution(mesh):
    return jax.shard_map(
        local,
        mesh=mesh,
        in_specs=(P(None, "orb", "walk"), P(), P("walk", None, None), P("orb")),
        out_specs=(P("walk", "orb"), P("orb", None, "walk")),
        check_vma=False,
    )
```

time: 106 us -> 57.2 us (0.54)
  blocking collectives: 64.2 us -> 0 us
  Pallas kernels: 0 us -> 53 us
  other arithmetic: 12.7 us -> 0 us
  matrix products: 11.7 us -> 0 us
  local copies, waits for them, and re-layouts: 10.8 us -> 3.38 us
  starting transfers between devices: 4.04 us -> 0 us
    pallas_call x0 -> x1, Pallas kernels: none -> 53 us  [local(): pl.pallas_call(kernel, out_shape=(jax.ShapeDtypeStruct((1, 4), F32), jax....]
    all_to_all x2 -> x0, blocking collectives: 41.2 us -> none  [the longest x1 28.6 us: local(): lax.all_to_all(products.astype(jnp.bfloat16), WALK, split_axis=2, concat_...]
    unnamed x2 -> x0, blocking collectives: 23 us -> none
    dot_general x3 -> x0, matrix products: 11.7 us -> none  [the longest x1 4.52 us: local(): jnp.einsum('pi,gpq->giq', orbitals, regrouped, preferred_element_type=jnp...]
    unnamed x1 -> x0, other arithmetic: 11.5 us -> none
    all_to_all x3 -> x0, local copies, waits for them, and re-layouts: 6.17 us -> none  [the longest x2 5.74 us: local(): lax.all_to_all(chol, 'orb', split_axis=0, concat_axis=1, tiled=True)]
    all_to_all x1 -> x0, starting transfers between devices: 4.04 us -> none  [local(): lax.all_to_all(chol, 'orb', split_axis=0, concat_axis=1, tiled=True)]
    sub x1 -> x0, other arithmetic: 1.16 us -> none  [local(): return (totals - shift[None, :], rotated)]
  transfers between devices with their start and end apart: 1 -> 0, of which waited for: 1 -> 0; matrix products, arithmetic and copies ran while one was open for 2% -> 0% of each run, Pallas kernels for 0% -> 0%
where the time goes in v1:
time: 57.2 us; the launch traced here: 57.1 us
  Pallas kernels  53 us (93%)
  local copies, waits for them, and re-layouts  3.38 us (6%)
  between operations  0.64 us (1%)
    pallas_call x1, Pallas kernels, local(): pl.pallas_call(kernel, out_shape=(jax.ShapeDtypeStruct((1, 4), F32), jax....  53 us
    unnamed x2, local copies, waits for them, and re-layouts  3.38 us

profile of v1, /device:TPU:1, one launch (start us, length us, event | category | flops | bytes accessed | tf_op | source)
XLA Modules:
  0.0 57.1 jit_solution(6370372251890017629)
XLA Ops:
  0.6 53.0 %half_rotation.1 = (f32[1,4]{1,0:T(1,128)}, bf16[4,1024,128]{2,1,0:T(8,128)(2,1)}) custom-call(bf16[64,128,128]{2,1,0:T(8,128)(2,1)} %chol.1, bf16[2048,1024]{1,0:T(8,128)(2,1)} %orbitals.1, bf16[1,1024,2048]{2,1,0:T(8,128)(2,1)} %greens.1, f32[4]{0:T(128)} %shift.1), custom_call_target="tpu_custom_call" | custom-call | tf_op jit(solution)/shard_map/half_rotation/pallas_call | solution.py:289
  53.7 1.1 %copy.8 = f32[1,4]{1,0:T(1,128)} copy(f32[1,4]{1,0:T(1,128)} %get-tuple-element.4) | data formatting | bytes 32
  54.8 2.3 %copy.9 = bf16[4,1024,128]{2,1,0:T(8,128)(2,1)} copy(bf16[4,1024,128]{2,1,0:T(8,128)(2,1)} %get-tuple-element.5) | data formatting | bytes 2097152

commit v2 on v1

--- a/solution.py
+++ b/solution.py
@@ -8,11 +8,9 @@
 MESH = pl.DeviceIdType.MESH
 F32, BF16 = jnp.float32, jnp.bfloat16
 FAR_FIRST = (4, 3, 5, 2, 6, 1, 7, 0)
-CHIPS = ((0, 0), (1, 0), (3, 0), (2, 0), (2, 1), (1, 1), (3, 1), (0, 1))
-
 
 def kernel(
-    chol, orbitals, greens, shift, fb_out, rot_out,
+    chol, orbitals, greens, fb_out, rot_out,
     rows_v, greens_v, orb_v, orb_t, chol_v, chunks, acc,
     t_out, t_in, diag, part_out, part_in, sum_out, sum_in,
     orb_ready, walk_ready, load_sem, greens_sem,
@@ -42,11 +40,14 @@
     def loop(start, stop, body):
         lax.fori_loop(start, stop, lambda i, _: body(i), None)
 
+    es = jax.named_scope('e_sig'); es.__enter__()
     barrier = pltpu.get_barrier_semaphore()
     signal(barrier, place(partner, w))
     loop(pair + 2, 16, lambda i: signal(barrier, place(i, w)))
     loop(w + 1, 16, lambda i: signal(barrier, met(i)))
 
+    es.__exit__(None,None,None)
+    es = jax.named_scope('e_load'); es.__enter__()
     own_rows = pltpu.make_async_copy(
         orbitals.at[pl.ds(pl.multiple_of(o * 128, 128), 128)], rows_v.at[h], load_sem.at[0]
     )
@@ -70,9 +71,11 @@
     own_chunk = pltpu.make_async_copy(chol.at[pl.ds(4 * o, 4)], chunks.at[o], load_sem.at[4])
     own_chunk.start()
 
-    pl.semaphore_wait(barrier, pair + 1 + w)
+    es.__exit__(None,None,None)
+    with jax.named_scope("w_bar"):
+        pl.semaphore_wait(barrier, pair + 1 + w)
+    loop(0, w, lambda i: signal(walk_ready.at[w // 8], met(i)))
     loop(0, pair, lambda i: signal(orb_ready, place(i, w)))
-    loop(0, w, lambda i: signal(walk_ready, met(i)))
 
     def chunk_copy(to):
         return pltpu.make_async_remote_copy(
@@ -97,22 +100,39 @@
     def chip(dy, da):
         return ((y + dy) % 4) * 2 + (a + da) % 2
 
-    await_some(orb_ready, 14 - pair)
-    for dy, da in ((2, 1), (1, 1), (3, 1), (0, 1), (2, 0), (1, 0), (3, 0)):
-        for dc in range(2):
-            chunk_copy(chip(dy, da) * 2 + (c + dc) % 2).start()
-    chunk_copy(partner).start()
-
-    own_rows.wait()
-    far_rows.wait()
-    for k, dz in enumerate(FAR_FIRST):
-        columns[k].wait()
-        there = (z + dz) % 8
-        both = jnp.dot(
-            rows_v[...].reshape(256, 1024), greens_v[k], preferred_element_type=F32
-        ).astype(BF16)
-        t_out[2 * there] = both[:128, :128]
-        t_out[2 * there + 1] = both[128:, 128:]
+    order = ((2, 1), (1, 1), (3, 1), (0, 1), (2, 0), (1, 0), (3, 0))
+
+    def scatter_all():
+        with jax.named_scope("w_orb"):
+            await_some(orb_ready, 14 - pair)
+        for dy, da in order:
+            for dc in range(2):
+                chunk_copy(chip(dy, da) * 2 + (c + dc) % 2).start()
+        chunk_copy(partner).start()
+
+    def products():
+        own_rows.wait()
+        far_rows.wait()
+        for k, dz in enumerate(FAR_FIRST):
+            columns[k].wait()
+            there = (z + dz) % 8
+            both = jnp.dot(
+                rows_v[...].reshape(256, 1024), greens_v[k], preferred_element_type=F32
+            ).astype(BF16)
+            t_out[2 * there] = both[:128, :128]
+            t_out[2 * there + 1] = both[128:, 128:]
+
+    @pl.when(y < 2)
+    def _():
+        with jax.named_scope("prod"):
+            products()
+        scatter_all()
+
+    @pl.when(y >= 2)
+    def _():
+        scatter_all()
+        with jax.named_scope("prod"):
+            products()
 
     def t_copy(to, source):
         return pltpu.make_async_remote_copy(
@@ -124,11 +144,21 @@
             device_id_type=MESH,
         )
 
-    await_some(walk_ready, 15 - w)
-    for dz in FAR_FIRST:
-        for dh in (1, 0):
-            if dz or dh:
-                t_copy(((z + dz) % 8) * 2 + (h + dh) % 2, w).start()
+    def send_products(wanted):
+        for dz in FAR_FIRST:
+            for dh in (1, 0):
+                to = ((z + dz) % 8) * 2 + (h + dh) % 2
+
+                @pl.when(wanted(to))
+                def _():
+                    t_copy(to, w).start()
+
+    with jax.named_scope("w_walk0"):
+        await_some(walk_ready.at[0], 7 - w)
+    send_products(lambda to: (to < 8) & (to != w))
+    with jax.named_scope("w_walk1"):
+        await_some(walk_ready.at[1], jnp.where(w < 8, 8, 15 - w))
+    send_products(lambda to: (to >= 8) & (to != w))
     t_in[w] = t_out[w]
 
     all_rows.wait()
@@ -137,38 +167,44 @@
         at = pl.ds(pl.multiple_of(i * 128, 128), 128)
         orb_t[:, at] = orb_v[at, :].T
 
-    loop(0, 16, turn)
-
-    def rotate(which):
-        dy, da = CHIPS[which]
-        there = chip(dy, da)
-        if which == 0:
-            own_chunk.wait()
-            chunk_arrival(partner)
-        else:
-            chunk_arrival(2 * there)
-            chunk_arrival(2 * there + 1)
-        block = jnp.concatenate(
-            [
-                jnp.concatenate([chunks[2 * there, g], chunks[2 * there + 1, g]], axis=0)
-                for g in range(4)
-            ],
-            axis=1,
-        )
-        at = pl.ds(pl.multiple_of(there * 256, 256), 256)
-
-        def rows(i):
-            here = pl.ds(pl.multiple_of(i * 256, 256), 256)
-            term = jnp.dot(orb_t[here, at], block, preferred_element_type=F32)
-            if which:
-                term = acc[here, :] + term
-            if which < 7:
-                acc[here, :] = term
-            else:
-                for g in range(4):
-                    rot_out[g, here, :] = term[:, g * 128 : (g + 1) * 128].astype(BF16)
-
-        loop(0, 4, rows)
+    with jax.named_scope("turn"):
+        loop(0, 16, turn)
+
+    def rotate(group, first=False, last=False):
+        spots = []
+        for dy, da in group:
+            there = chip(dy, da)
+            with jax.named_scope(f"w_c{dy}{da}"):
+                if dy or da:
+                    chunk_arrival(2 * there)
+                    chunk_arrival(2 * there + 1)
+                else:
+                    own_chunk.wait()
+                    chunk_arrival(partner)
+            spots.append(there)
+        with jax.named_scope(f"rot{group[0][0]}{group[0][1]}"):
+            left = jnp.concatenate(
+                [orb_t[:, pl.ds(pl.multiple_of(there * 256, 256), 256)] for there in spots], axis=1
+            )
+            for n in range(2):
+                block = jnp.concatenate(
+                    [
+                        jnp.concatenate(
+                            [chunks[2 * there + i, g] for there in spots for i in range(2)], axis=0
+                        )
+                        for g in (2 * n, 2 * n + 1)
+                    ],
+                    axis=1,
+                )
+                term = jnp.dot(left, block, preferred_element_type=F32)
+                at = slice(256 * n, 256 * n + 256)
+                if not first:
+                    term = acc[:, at] + term
+                if last:
+                    rot_out[2 * n] = term[:, :128].astype(BF16)
+                    rot_out[2 * n + 1] = term[:, 128:].astype(BF16)
+                else:
+                    acc[:, at] = term
 
     lane = lax.broadcasted_iota(jnp.int32, (256, 128), 1)
     row = lax.broadcasted_iota(jnp.int32, (256, 128), 0)
@@ -185,18 +221,20 @@
         )
 
     def terms(first):
-        for k in range(first, first + 8):
+        with jax.named_scope(f"w_t{first}"):
+          for k in range(first, first + 8):
             @pl.when(w != k)
             def _():
                 t_copy(k, k).wait_recv()
+        tsc = jax.named_scope(f"terms{first}"); tsc.__enter__()
 
         right = jnp.concatenate(
             [t_in[first : first + 8, 16 * b : 16 * b + 16, :].reshape(128, 128) for b in range(8)],
             axis=1,
         )
 
-        def vectors(j):
-            at = pl.ds(pl.multiple_of(j * 16, 16), 16)
+        for j in range(4):
+            at = slice(16 * j, 16 * j + 16)
             left = jnp.concatenate(
                 [chol_v[at, 16 * b : 16 * b + 16, :].reshape(256, 128) for b in range(8)],
                 axis=1,
@@ -207,7 +245,6 @@
             kept = jnp.where(same_row, product, 0.0)
             diag[at, :] = kept.reshape(16, 16, 128).sum(axis=1)
 
-        loop(0, 4, vectors)
         picks = jnp.where(
             lax.broadcasted_iota(jnp.int32, (8, 128), 1) // 16
             == lax.broadcasted_iota(jnp.int32, (8, 128), 0),
@@ -223,19 +260,18 @@
             @pl.when(w != k)
             def _():
                 part_copy(k, w).start()
+        tsc.__exit__(None,None,None)
 
     diag[64:, :] = jnp.zeros((64, 128), F32)
-    for which in range(4):
-        rotate(which)
+    rotate(((0, 0),), first=True)
     own_chol.wait()
     terms(0)
-    rotate(4)
     terms(8)
-    rotate(5)
-    rotate(6)
-
+    rotate(((2, 0), (2, 1)))
+    rotate(((1, 1), (3, 1)))
     part_in[w] = part_out[w]
-    for k in range(16):
+    with jax.named_scope("w_part"):
+      for k in range(16):
         @pl.when(w != k)
         def _():
             part_copy(k, k).wait_recv()
@@ -257,20 +293,18 @@
         def _():
             sum_copy(k, o).start()
     sum_in[o] = sum_out[...]
-    rotate(7)
-    for k in range(16):
+    rotate(((1, 0), (3, 0), (0, 1)), last=True)
+    with jax.named_scope("w_sum"):
+      for k in range(16):
         @pl.when(o != k)
         def _():
             sum_copy(k, k).wait_recv()
 
     total = pltpu.roll(sum_in[...].sum(axis=0), (128 - 4 * o) % 128, 1)[:1]
-    spot = lax.broadcasted_iota(jnp.int32, (1, 128), 1)
-    moved = jnp.zeros((1, 128), F32)
-    for j in range(4):
-        moved = jnp.where(spot == j, shift[j], moved)
-    fb_out[...] = (total - moved)[:, :4]
-
-    for k in range(16):
+    fb_out[...] = total[:, :4]
+
+    with jax.named_scope("w_send"):
+      for k in range(16):
         @pl.when(o != k)
         def _():
             chunk_copy(k).wait_send()
@@ -283,16 +317,16 @@
 
 
 def local(chol, orbitals, greens, shift):
-    anywhere = pl.BlockSpec(memory_space=pl.ANY)
+    anywhere = pl.BlockSpec(memory_space=pltpu.HBM)
     in_vmem = pl.BlockSpec(memory_space=pltpu.VMEM)
     sems = [pltpu.SemaphoreType.DMA((16,))] * 8
-    return pl.pallas_call(
+    force_bias, rotated = pl.pallas_call(
         kernel,
         out_shape=(
             jax.ShapeDtypeStruct((1, 4), F32),
             jax.ShapeDtypeStruct((4, 1024, 128), BF16),
         ),
-        in_specs=[anywhere, anywhere, anywhere, pl.BlockSpec(memory_space=pltpu.SMEM)],
+        in_specs=[anywhere] * 3,
         out_specs=(in_vmem, in_vmem),
         scratch_shapes=[
             pltpu.VMEM((2, 128, 1024), BF16),
@@ -310,16 +344,17 @@
             pltpu.VMEM((8, 128), F32),
             pltpu.VMEM((16, 8, 128), F32),
             pltpu.SemaphoreType.REGULAR,
-            pltpu.SemaphoreType.REGULAR,
+            pltpu.SemaphoreType.REGULAR((2,)),
             pltpu.SemaphoreType.DMA((5,)),
             pltpu.SemaphoreType.DMA((8,)),
             *sems,
         ],
         compiler_params=pltpu.CompilerParams(
-            collective_id=0, has_side_effects=True, vmem_limit_bytes=62 * 2**20
+            collective_id=0, has_side_effects=True, vmem_limit_bytes=52 * 2**20
         ),
         name="half_rotation",
-    )(chol, orbitals, greens, shift)
+    )(chol, orbitals, greens)
+    return force_bias - shift[None, :], rotated
 
 
 def solution(mesh):

time: 57.2 us -> 41.9 us (0.73)
  Pallas kernels: 53 us -> 39.6 us
  local copies, waits for them, and re-layouts: 3.38 us -> 0.97 us
    pallas_call x1, Pallas kernels: 53 us -> 39.6 us  [local(): pl.pallas_call(kernel, out_shape=(jax.ShapeDtypeStruct((1, 4), F32), jax....]
    unnamed x2 -> x3, local copies, waits for them, and re-layouts: 3.38 us -> 0.97 us
where the time goes in v2:
time: 41.9 us; the launch traced here: 41.8 us
  Pallas kernels  39.6 us (95%)
  local copies, waits for them, and re-layouts  0.97 us (2%)
  between operations  0.65 us (2%)
  other arithmetic  0.51 us (1%)
    pallas_call x1, Pallas kernels, local(): pl.pallas_call(kernel, out_shape=(jax.ShapeDtypeStruct((1, 4), F32), jax....  39.6 us
    unnamed x3, local copies, waits for them, and re-layouts  0.97 us

profile of v2, /device:TPU:1, one launch (start us, length us, event | category | flops | bytes accessed | tf_op | source)
XLA Modules:
  0.0 41.8 jit_solution(4597062982885883745)
XLA Ops:
  0.6 0.0 copy-start
  0.6 39.6 %half_rotation.1 = (f32[1,4]{1,0:T(1,128)S(1)}, bf16[4,1024,128]{2,1,0:T(8,128)(2,1)S(1)}) custom-call(bf16[64,128,128]{2,1,0:T(8,128)(2,1)} %chol.1, bf16[2048,1024]{1,0:T(8,128)(2,1)} %orbitals.1, bf16[1,1024,2048]{2,1,0:T(8,128)(2,1)} %greens.1), custom_call_target="tpu_custom_call" | custom-call | tf_op jit(solution)/shard_map/half_rotation/pallas_call | solution.py:323
  40.3 0.0 copy-done
  40.3 0.5 %bitcast_subtract_fusion = f32[1,4]{1,0:T(1,128)} fusion(f32[1,4]{1,0:T(1,128)S(1)} %get-tuple-element.4, f32[4]{0:T(128)S(1)} %copy-done), kind=kLoop, calls=%fused_computation | loop fusion | flops 4 | bytes 48 | tf_op jit(solution)/shard_map/sub | solution.py:357
  40.8 1.0 %copy.7 = bf16[4,1024,128]{2,1,0:T(8,128)(2,1)} copy(bf16[4,1024,128]{2,1,0:T(8,128)(2,1)S(1)} %get-tuple-element.9) | data formatting | bytes 2097152
Async XLA Ops:
  0.6 39.7 %copy-start = (f32[4]{0:T(128)S(1)}, f32[4]{0:T(128)}, u32[]{:S(2)}) copy-start(f32[4]{0:T(128)} %param.7) | copy-start | bytes 52

commit v3 on v2

--- a/solution.py
+++ b/solution.py
@@ -12,7 +12,7 @@
 def kernel(
     chol, orbitals, greens, fb_out, rot_out,
     rows_v, greens_v, orb_v, orb_t, chol_v, chunks, acc,
-    t_out, t_in, diag, part_out, part_in, sum_out, sum_in,
+    t_out, t_in, diag_few, diag_all, part_out, part_in, sum_out, sum_in,
     orb_ready, walk_ready, load_sem, greens_sem,
     chol_send, chol_recv, t_send, t_recv, part_send, part_recv, sum_send, sum_recv,
 ):
@@ -42,9 +42,10 @@
 
     es = jax.named_scope('e_sig'); es.__enter__()
     barrier = pltpu.get_barrier_semaphore()
+    loop(8, jnp.where(z < 4, 16, 0), lambda i: signal(barrier, met(i)))
     signal(barrier, place(partner, w))
     loop(pair + 2, 16, lambda i: signal(barrier, place(i, w)))
-    loop(w + 1, 16, lambda i: signal(barrier, met(i)))
+    loop(w + 1, 8, lambda i: signal(barrier, met(i)))
 
     es.__exit__(None,None,None)
     es = jax.named_scope('e_load'); es.__enter__()
@@ -64,17 +65,10 @@
         )
         copy.start()
         columns.append(copy)
-    all_rows = pltpu.make_async_copy(orbitals, orb_v, load_sem.at[2])
-    all_rows.start()
-    own_chol = pltpu.make_async_copy(chol, chol_v, load_sem.at[3])
-    own_chol.start()
-    own_chunk = pltpu.make_async_copy(chol.at[pl.ds(4 * o, 4)], chunks.at[o], load_sem.at[4])
-    own_chunk.start()
-
     es.__exit__(None,None,None)
     with jax.named_scope("w_bar"):
-        pl.semaphore_wait(barrier, pair + 1 + w)
-    loop(0, w, lambda i: signal(walk_ready.at[w // 8], met(i)))
+        pl.semaphore_wait(barrier, pair + 1 + jnp.minimum(w, 8))
+    loop(0, jnp.minimum(w, 8), lambda i: signal(walk_ready.at[w // 8], met(i)))
     loop(0, pair, lambda i: signal(orb_ready, place(i, w)))
 
     def chunk_copy(to):
@@ -110,29 +104,9 @@
                 chunk_copy(chip(dy, da) * 2 + (c + dc) % 2).start()
         chunk_copy(partner).start()
 
-    def products():
-        own_rows.wait()
-        far_rows.wait()
-        for k, dz in enumerate(FAR_FIRST):
-            columns[k].wait()
-            there = (z + dz) % 8
-            both = jnp.dot(
-                rows_v[...].reshape(256, 1024), greens_v[k], preferred_element_type=F32
-            ).astype(BF16)
-            t_out[2 * there] = both[:128, :128]
-            t_out[2 * there + 1] = both[128:, 128:]
-
-    @pl.when(y < 2)
-    def _():
-        with jax.named_scope("prod"):
-            products()
-        scatter_all()
-
-    @pl.when(y >= 2)
-    def _():
-        scatter_all()
-        with jax.named_scope("prod"):
-            products()
+    all_rows = pltpu.make_async_copy(orbitals, orb_v, load_sem.at[2])
+    own_chol = pltpu.make_async_copy(chol, chol_v, load_sem.at[3])
+    own_chunk = pltpu.make_async_copy(chol.at[pl.ds(4 * o, 4)], chunks.at[o], load_sem.at[4])
 
     def t_copy(to, source):
         return pltpu.make_async_remote_copy(
@@ -153,13 +127,58 @@
                 def _():
                     t_copy(to, w).start()
 
+    own_rows.wait()
+    far_rows.wait()
+
+    def products(start, stop):
+        for k in range(start, stop):
+            columns[k].wait()
+        for k in range(start, stop):
+            there = (z + FAR_FIRST[k]) % 8
+            both = jnp.dot(
+                rows_v[...].reshape(256, 1024), greens_v[k], preferred_element_type=F32
+            ).astype(BF16)
+            t_out[2 * there] = both[:128, :128]
+            t_out[2 * there + 1] = both[128:, 128:]
+
+    def all_products():
+        with jax.named_scope("prod1"):
+            products(0, 4)
+        all_rows.start()
+        own_chol.start()
+        own_chunk.start()
+        with jax.named_scope("prod"):
+            products(4, 8)
+
+        @pl.when(z >= 4)
+        def _():
+            send_products(lambda to: to < 8)
+
+    @pl.when(y < 2)
+    def _():
+        all_products()
+        scatter_all()
+
+    @pl.when(y >= 2)
+    def _():
+        scatter_all()
+        all_products()
+
+    def products_from(first, count):
+        for k in range(first, first + count):
+
+            @pl.when(w != k)
+            def _():
+                t_copy(k, k).wait_recv()
+
+    patient = (z == 2) | (z == 3)
     with jax.named_scope("w_walk0"):
         await_some(walk_ready.at[0], 7 - w)
-    send_products(lambda to: (to < 8) & (to != w))
-    with jax.named_scope("w_walk1"):
-        await_some(walk_ready.at[1], jnp.where(w < 8, 8, 15 - w))
-    send_products(lambda to: (to >= 8) & (to != w))
-    t_in[w] = t_out[w]
+
+    @pl.when(z < 4)
+    def _():
+        send_products(lambda to: (to < 8) & (to != w))
+
 
     all_rows.wait()
 
@@ -169,6 +188,27 @@
 
     with jax.named_scope("turn"):
         loop(0, 16, turn)
+
+    @pl.when(patient)
+    def _():
+        with jax.named_scope("w_pat"):
+            products_from(0, 2)
+
+    with jax.named_scope("w_walk1"):
+        @pl.when(z < 4)
+        def _():
+            pl.semaphore_wait(walk_ready.at[1], 8)
+
+        @pl.when(w == 7)
+        def _():
+            loop(8, 16, lambda i: signal(walk_ready.at[0], met(i)))
+
+        @pl.when(z >= 4)
+        def _():
+            pl.semaphore_wait(walk_ready.at[0], 1)
+
+    send_products(lambda to: (to >= 8) & (to != w))
+    t_in[w] = t_out[w]
 
     def rotate(group, first=False, last=False):
         spots = []
@@ -206,10 +246,6 @@
                 else:
                     acc[:, at] = term
 
-    lane = lax.broadcasted_iota(jnp.int32, (256, 128), 1)
-    row = lax.broadcasted_iota(jnp.int32, (256, 128), 0)
-    same_row = (lane % 16) == (row % 16)
-
     def part_copy(to, source):
         return pltpu.make_async_remote_copy(
             src_ref=part_out.at[to],
@@ -220,19 +256,15 @@
             device_id_type=MESH,
         )
 
-    def terms(first):
-        with jax.named_scope(f"w_t{first}"):
-          for k in range(first, first + 8):
-            @pl.when(w != k)
-            def _():
-                t_copy(k, k).wait_recv()
-        tsc = jax.named_scope(f"terms{first}"); tsc.__enter__()
-
+    def terms(count, skipped, diag):
+        lanes = 16 * count
         right = jnp.concatenate(
-            [t_in[first : first + 8, 16 * b : 16 * b + 16, :].reshape(128, 128) for b in range(8)],
-            axis=1,
-        )
-
+            [t_in[:count, 16 * b : 16 * b + 16, :].reshape(lanes, 128) for b in range(8)], axis=1
+        )
+        same_row = (
+            lax.broadcasted_iota(jnp.int32, (256, lanes), 1) % 16
+            == lax.broadcasted_iota(jnp.int32, (256, lanes), 0) % 16
+        )
         for j in range(4):
             at = slice(16 * j, 16 * j + 16)
             left = jnp.concatenate(
@@ -242,33 +274,43 @@
             product = lax.dot_general(
                 left, right, (((1,), (1,)), ((), ())), preferred_element_type=F32
             )
-            kept = jnp.where(same_row, product, 0.0)
-            diag[at, :] = kept.reshape(16, 16, 128).sum(axis=1)
+            diag[at, :] = jnp.where(same_row, product, 0.0).reshape(16, 16, lanes).sum(axis=1)
 
         picks = jnp.where(
-            lax.broadcasted_iota(jnp.int32, (8, 128), 1) // 16
-            == lax.broadcasted_iota(jnp.int32, (8, 128), 0),
+            lax.broadcasted_iota(jnp.int32, (16, lanes), 1) // 16
+            == lax.broadcasted_iota(jnp.int32, (16, lanes), 0),
             1.0, 0.0,
         )
         sums = lax.dot_general(
             picks, diag[...], (((1,), (1,)), ((), ())),
             precision=lax.Precision.HIGHEST, preferred_element_type=F32,
         )
-        for k in range(8):
-            part_out[first + k] = jnp.broadcast_to(sums[k : k + 1, :], (8, 128))
-        for k in range(first, first + 8):
+        for k in range(skipped, count):
+            part_out[k] = jnp.broadcast_to(sums[k : k + 1, :], (8, 128))
+        for k in range(skipped, count):
+
             @pl.when(w != k)
             def _():
                 part_copy(k, w).start()
-        tsc.__exit__(None,None,None)
-
-    diag[64:, :] = jnp.zeros((64, 128), F32)
+
+    diag_few[64:, :] = jnp.zeros((64, 64), F32)
+    diag_all[64:, :] = jnp.zeros((64, 256), F32)
     rotate(((0, 0),), first=True)
     own_chol.wait()
-    terms(0)
-    terms(8)
-    rotate(((2, 0), (2, 1)))
-    rotate(((1, 1), (3, 1)))
+    with jax.named_scope("w_t0"):
+
+        @pl.when(jnp.logical_not(patient))
+        def _():
+            products_from(0, 2)
+
+        products_from(2, 2)
+
+    with jax.named_scope("terms0"):
+        terms(4, 0, diag_few)
+    with jax.named_scope("w_t4"):
+        products_from(4, 12)
+    with jax.named_scope("terms4"):
+        terms(16, 4, diag_all)
     part_in[w] = part_out[w]
     with jax.named_scope("w_part"):
       for k in range(16):
@@ -293,6 +335,8 @@
         def _():
             sum_copy(k, o).start()
     sum_in[o] = sum_out[...]
+    rotate(((2, 0), (2, 1)))
+    rotate(((1, 1), (3, 1)))
     rotate(((1, 0), (3, 0), (0, 1)), last=True)
     with jax.named_scope("w_sum"):
       for k in range(16):
@@ -314,6 +358,19 @@
         def _():
             t_copy(k, w).wait_send()
             part_copy(k, w).wait_send()
+
+
+def finish(total, shift, rotated, fb_out, rot_out, fb_v, sems):
+    copies = [
+        pltpu.make_async_copy(rotated.at[g], rot_out.at[g], sems.at[g]) for g in range(4)
+    ]
+    for copy in copies:
+        copy.start()
+    fb_v[...] = total[...] - shift[...]
+    copies.append(pltpu.make_async_copy(fb_v, fb_out, sems.at[4]))
+    copies[4].start()
+    for copy in copies:
+        copy.wait()
 
 
 def local(chol, orbitals, greens, shift):
@@ -338,7 +395,8 @@
             pltpu.VMEM((1024, 512), F32),
             pltpu.VMEM((16, 128, 128), BF16),
             pltpu.VMEM((16, 128, 128), BF16),
-            pltpu.VMEM((128, 128), F32),
+            pltpu.VMEM((128, 64), F32),
+            pltpu.VMEM((128, 256), F32),
             pltpu.VMEM((16, 8, 128), F32),
             pltpu.VMEM((16, 8, 128), F32),
             pltpu.VMEM((8, 128), F32),
@@ -354,7 +412,18 @@
         ),
         name="half_rotation",
     )(chol, orbitals, greens)
-    return force_bias - shift[None, :], rotated
+    return pl.pallas_call(
+        finish,
+        out_shape=(
+            jax.ShapeDtypeStruct((1, 4), F32),
+            jax.ShapeDtypeStruct((4, 1024, 128), BF16),
+        ),
+        in_specs=[in_vmem] * 3,
+        out_specs=(anywhere, anywhere),
+        scratch_shapes=[pltpu.VMEM((1, 4), F32), pltpu.SemaphoreType.DMA((5,))],
+        compiler_params=pltpu.CompilerParams(vmem_limit_bytes=2**20),
+        name="finish",
+    )(force_bias, shift.reshape(1, 4), rotated)
 
 
 def solution(mesh):

time: 41.9 us -> 39.8 us (0.950)
  local copies, waits for them, and re-layouts: 0.97 us -> 0.01 us
  Pallas kernels: 39.6 us -> 39 us
  other arithmetic: 0.51 us -> 0 us
    pallas_call x1, Pallas kernels: 39.6 us -> 38 us  [local(): pl.pallas_call(kernel, out_shape=(jax.ShapeDtypeStruct((1, 4), F32), jax....]
    pallas_call x0 -> x1, Pallas kernels: none -> 1.01 us  [local(): pl.pallas_call(finish, out_shape=(jax.ShapeDtypeStruct((1, 4), F32), jax....]
    unnamed x3 -> x2, local copies, waits for them, and re-layouts: 0.97 us -> 0.01 us
    sub x1 -> x0, other arithmetic: 0.51 us -> none  [local(): return (force_bias - shift[None, :], rotated)]
where the time goes in v3:
time: 39.8 us; the launch traced here: 39.7 us
  Pallas kernels  39 us (98%)
  between operations  0.65 us (2%)
    pallas_call x1, Pallas kernels, local(): pl.pallas_call(kernel, out_shape=(jax.ShapeDtypeStruct((1, 4), F32), jax....  38 us
    pallas_call x1, Pallas kernels, local(): pl.pallas_call(finish, out_shape=(jax.ShapeDtypeStruct((1, 4), F32), jax....  1.01 us

profile of v3, /device:TPU:1, one launch (start us, length us, event | category | flops | bytes accessed | tf_op | source)
XLA Modules:
  0.0 39.7 jit_solution(4768950206368510152)
XLA Ops:
  0.6 0.0 copy-start
  0.6 38.0 %half_rotation.1 = (f32[1,4]{1,0:T(1,128)S(1)}, bf16[4,1024,128]{2,1,0:T(8,128)(2,1)S(1)}) custom-call(bf16[64,128,128]{2,1,0:T(8,128)(2,1)} %chol.1, bf16[2048,1024]{1,0:T(8,128)(2,1)} %orbitals.1, bf16[1,1024,2048]{2,1,0:T(8,128)(2,1)} %greens.1), custom_call_target="tpu_custom_call" | custom-call | tf_op jit(solution)/shard_map/half_rotation/pallas_call | solution.py:380
  38.7 0.0 copy-done
  38.7 1.0 %finish.1 = (f32[1,4]{1,0:T(1,128)}, bf16[4,1024,128]{2,1,0:T(8,128)(2,1)}) custom-call(f32[1,4]{1,0:T(1,128)S(1)} %get-tuple-element.4.total, f32[1,4]{1,0:T(1,128)S(1)} %bitcast.1, bf16[4,1024,128]{2,1,0:T(8,128)(2,1)S(1)} %get-tuple-element.5.rotated), custom_call_target="tpu_custom_call" | custom-call | tf_op jit(solution)/shard_map/finish/pallas_call | solution.py:415
Async XLA Ops:
  0.6 38.1 %copy-start = (f32[4]{0:T(128)S(1)}, f32[4]{0:T(128)}, u32[]{:S(2)}) copy-start(f32[4]{0:T(128)} %param.7) | copy-start | bytes 52

commit v4 on v3

--- a/solution.py
+++ b/solution.py
@@ -286,7 +286,7 @@
             precision=lax.Precision.HIGHEST, preferred_element_type=F32,
         )
         for k in range(skipped, count):
-            part_out[k] = jnp.broadcast_to(sums[k : k + 1, :], (8, 128))
+            part_out[k] = sums[k : k + 1, :]
         for k in range(skipped, count):
 
             @pl.when(w != k)
@@ -330,10 +330,11 @@
             device_id_type=MESH,
         )
 
-    for k in range(16):
-        @pl.when(o != k)
-        def _():
-            sum_copy(k, o).start()
+    for dy in (2, 1, 3, 0):
+        for da in (1, 0):
+            for dc in range(2):
+                if dy or da or dc:
+                    sum_copy(chip(dy, da) * 2 + (c + dc) % 2, o).start()
     sum_in[o] = sum_out[...]
     rotate(((2, 0), (2, 1)))
     rotate(((1, 1), (3, 1)))
@@ -397,10 +398,10 @@
             pltpu.VMEM((16, 128, 128), BF16),
             pltpu.VMEM((128, 64), F32),
             pltpu.VMEM((128, 256), F32),
-            pltpu.VMEM((16, 8, 128), F32),
-            pltpu.VMEM((16, 8, 128), F32),
-            pltpu.VMEM((8, 128), F32),
-            pltpu.VMEM((16, 8, 128), F32),
+            pltpu.VMEM((16, 1, 128), F32),
+            pltpu.VMEM((16, 1, 128), F32),
+            pltpu.VMEM((1, 128), F32),
+            pltpu.VMEM((16, 1, 128), F32),
             pltpu.SemaphoreType.REGULAR,
             pltpu.SemaphoreType.REGULAR((2,)),
             pltpu.SemaphoreType.DMA((5,)),

time: 39.8 us -> 39.4 us (0.990)
  Pallas kernels: 39 us -> 38.6 us
    pallas_call x1, Pallas kernels: 38 us -> 37.6 us  [local(): pl.pallas_call(kernel, out_shape=(jax.ShapeDtypeStruct((1, 4), F32), jax....]
where the time goes in v4:
time: 39.4 us; the launch traced here: 39.3 us
  Pallas kernels  38.6 us (98%)
  between operations  0.65 us (2%)
    pallas_call x1, Pallas kernels, local(): pl.pallas_call(kernel, out_shape=(jax.ShapeDtypeStruct((1, 4), F32), jax....  37.6 us
    pallas_call x1, Pallas kernels, local(): pl.pallas_call(finish, out_shape=(jax.ShapeDtypeStruct((1, 4), F32), jax....  1.01 us

profile of v4, /device:TPU:1, one launch (start us, length us, event | category | flops | bytes accessed | tf_op | source)
XLA Modules:
  0.0 39.3 jit_solution(2677080804678099197)
XLA Ops:
  0.6 0.0 copy-start
  0.6 37.6 %half_rotation.1 = (f32[1,4]{1,0:T(1,128)S(1)}, bf16[4,1024,128]{2,1,0:T(8,128)(2,1)S(1)}) custom-call(bf16[64,128,128]{2,1,0:T(8,128)(2,1)} %chol.1, bf16[2048,1024]{1,0:T(8,128)(2,1)} %orbitals.1, bf16[1,1024,2048]{2,1,0:T(8,128)(2,1)} %greens.1), custom_call_target="tpu_custom_call" | custom-call | tf_op jit(solution)/shard_map/half_rotation/pallas_call | solution.py:381
  38.3 0.0 copy-done
  38.3 1.0 %finish.1 = (f32[1,4]{1,0:T(1,128)}, bf16[4,1024,128]{2,1,0:T(8,128)(2,1)}) custom-call(f32[1,4]{1,0:T(1,128)S(1)} %get-tuple-element.4.total, f32[1,4]{1,0:T(1,128)S(1)} %bitcast.1, bf16[4,1024,128]{2,1,0:T(8,128)(2,1)S(1)} %get-tuple-element.5.rotated), custom_call_target="tpu_custom_call" | custom-call | tf_op jit(solution)/shard_map/finish/pallas_call | solution.py:416
Async XLA Ops:
  0.6 37.6 %copy-start = (f32[4]{0:T(128)S(1)}, f32[4]{0:T(128)}, u32[]{:S(2)}) copy-start(f32[4]{0:T(128)} %param.7) | copy-start | bytes 52

commit v5 on v4

--- a/solution.py
+++ b/solution.py
@@ -339,6 +339,18 @@
     rotate(((2, 0), (2, 1)))
     rotate(((1, 1), (3, 1)))
     rotate(((1, 0), (3, 0), (0, 1)), last=True)
+    with jax.named_scope("w_send"):
+      for k in range(16):
+        @pl.when(o != k)
+        def _():
+            chunk_copy(k).wait_send()
+            sum_copy(k, o).wait_send()
+
+        @pl.when(w != k)
+        def _():
+            t_copy(k, w).wait_send()
+            part_copy(k, w).wait_send()
+
     with jax.named_scope("w_sum"):
       for k in range(16):
         @pl.when(o != k)
@@ -347,18 +359,6 @@
 
     total = pltpu.roll(sum_in[...].sum(axis=0), (128 - 4 * o) % 128, 1)[:1]
     fb_out[...] = total[:, :4]
-
-    with jax.named_scope("w_send"):
-      for k in range(16):
-        @pl.when(o != k)
-        def _():
-            chunk_copy(k).wait_send()
-            sum_copy(k, o).wait_send()
-
-        @pl.when(w != k)
-        def _():
-            t_copy(k, w).wait_send()
-            part_copy(k, w).wait_send()
 
 
 def finish(total, shift, rotated, fb_out, rot_out, fb_v, sems):

time: 39.4 us -> 39.3 us (level)
  no operation moved by 1% of the time
where the time goes in v5:
time: 39.3 us; the launch traced here: 39.2 us
  Pallas kernels  38.5 us (98%)
  between operations  0.65 us (2%)
    pallas_call x1, Pallas kernels, local(): pl.pallas_call(kernel, out_shape=(jax.ShapeDtypeStruct((1, 4), F32), jax....  37.5 us
    pallas_call x1, Pallas kernels, local(): pl.pallas_call(finish, out_shape=(jax.ShapeDtypeStruct((1, 4), F32), jax....  1.01 us

profile of v5, /device:TPU:1, one launch (start us, length us, event | category | flops | bytes accessed | tf_op | source)
XLA Modules:
  0.0 39.2 jit_solution(6457370183923026472)
XLA Ops:
  0.6 0.0 copy-start
  0.6 37.5 %half_rotation.1 = (f32[1,4]{1,0:T(1,128)S(1)}, bf16[4,1024,128]{2,1,0:T(8,128)(2,1)S(1)}) custom-call(bf16[64,128,128]{2,1,0:T(8,128)(2,1)} %chol.1, bf16[2048,1024]{1,0:T(8,128)(2,1)} %orbitals.1, bf16[1,1024,2048]{2,1,0:T(8,128)(2,1)} %greens.1), custom_call_target="tpu_custom_call" | custom-call | tf_op jit(solution)/shard_map/half_rotation/pallas_call | solution.py:381
  38.2 0.0 copy-done
  38.2 1.0 %finish.1 = (f32[1,4]{1,0:T(1,128)}, bf16[4,1024,128]{2,1,0:T(8,128)(2,1)}) custom-call(f32[1,4]{1,0:T(1,128)S(1)} %get-tuple-element.4.total, f32[1,4]{1,0:T(1,128)S(1)} %bitcast.1, bf16[4,1024,128]{2,1,0:T(8,128)(2,1)S(1)} %get-tuple-element.5.rotated), custom_call_target="tpu_custom_call" | custom-call | tf_op jit(solution)/shard_map/finish/pallas_call | solution.py:416
Async XLA Ops:
  0.6 37.5 %copy-start = (f32[4]{0:T(128)S(1)}, f32[4]{0:T(128)}, u32[]{:S(2)}) copy-start(f32[4]{0:T(128)} %param.7) | copy-start | bytes 52
